TPU v7x, 32 devices: a whole 2x2x4 slice. The times are simulated.
32 devices in a mesh: gx: 8 (over y, x, core), gy: 4 (over z).
Axes of the slice: x: 2, y: 2, z: 4, core: 2. Of those that a mesh axis runs over, the one named last changes fastest.
Arguments:
- probes: float32 [16, 128, 128, 256], P(None, 'gx', 'gy'), may hold values from -6 to 6
- diffusivity: float32 [128, 128, 256], P('gx', 'gy'), may hold values from 0.5 to 2
- wind_speed: float32 [3], replicated, may hold values from 0.5 to 2
- sensor_cell: int32 [8, 4, 128], P('gx', 'gy'), may hold values from 0 to 131071
- sensor_owner: int32 [8, 4, 128, 1], P('gx', 'gy'), may hold values from 0 to 31; in each aligned block of 128 rows (0 to 127, 128 to 255, ..., all dimensions but the last counted through in order) at most 4 rows name the same one
- sensor_count: int32 [8, 4], P('gx', 'gy'), may hold values from 64 to 128
- goal_weight: float32 [8, 4, 128, 16], P('gx', 'gy'), may hold values from -0.6 to 0.6
Outputs:
- fields: float32 [16, 128, 128, 256], P(None, 'gx', 'gy')
- goal_block: float32 [512, 16], P(('gx', 'gy'))
- ritz_gram: float32 [16, 16], replicated
Inputs may be any that keep to these rules, and one draw needn't show every extreme that they name: `sensor_owner`: among the rows of one device, no owner is named more than 4 times, a bound that some block reaches.
All inputs are finite; a program needn't handle non-finite values.
Results may differ from a plain program's by a relative error of at most 0.0003.
Values sent between devices are 32-bit elements; how exact they have to be, the bound alone decides.
A program may use at most 192 MiB of HBM per device.

v0:
```python
import jax
import jax.numpy as jnp
from jax import lax
from jax.sharding import PartitionSpec as P

STEPS = 2
SWEEPS = 4
time_step = 2.0


def padded_2(cells, sides, width):
    for axis, dim in sides:
        count = lax.axis_size(axis)
        ends = count - 1
        head = lax.slice_in_dim(cells, 0, width, axis=dim)
        tail = lax.slice_in_dim(cells, cells.shape[dim] - width, cells.shape[dim], axis=dim)
        cells = jnp.concatenate(
            [
                lax.ppermute(tail, axis, [(i, (i + 1) % count) for i in range(ends)]),
                cells,
                lax.ppermute(head, axis, [((i + 1) % count, i) for i in range(ends)]),
            ],
            axis=dim,
        )
    return cells


def relax(padded, source, diffusion, wind_speed):
    centre = padded[..., 1:-1, 1:-1, :]
    widths = [(0, 0)] * (centre.ndim - 1) + [(1, 1)]
    zpadded = jnp.pad(centre, widths)
    beside = padded[..., 2:, 1:-1, :] + padded[..., :-2, 1:-1, :]
    beside = beside + padded[..., 1:-1, 2:, :] + padded[..., 1:-1, :-2, :]
    beside = beside + zpadded[..., 2:] + zpadded[..., :-2]
    upwind = (
        wind_speed[0] * padded[..., :-2, 1:-1, :]
        + wind_speed[1] * padded[..., 1:-1, :-2, :]
        + wind_speed[2] * zpadded[..., :-2]
    )
    diagonal = 1.0 + time_step * (6.0 * diffusion + wind_speed[0] + wind_speed[1] + wind_speed[2])
    updated = (source + time_step * (diffusion * beside + upwind)) / diagonal
    return jnp.where(diffusion > 0.0, updated, 0.0)


def body(probes, diffusivity, wind_speed, sensor_cell, sensor_owner, sensor_count, goal_weight):
    state_field = probes
    for step_index in range(STEPS):
        source = state_field
        for sweep_index in range(SWEEPS):
            padded = padded_2(state_field, (("gx", 1), ("gy", 2)), 1)
            state_field = relax(padded, source, diffusivity, wind_speed)
    probe_count = state_field.shape[0]
    sensor_rows = sensor_cell.shape[2]
    goal_count = goal_weight.shape[3]
    device_count = lax.axis_size("gx") * lax.axis_size("gy")
    capacity = max(2, (sensor_rows + device_count - 1) // device_count)
    flattened = state_field.reshape(probe_count, -1)
    readings = jnp.take(flattened, sensor_cell.reshape(-1), axis=1)
    row_index = jnp.arange(sensor_rows, dtype=jnp.int32)
    active = (row_index < sensor_count.reshape(())).astype(jnp.float32)
    readings = readings.T * active[:, None]
    weights = goal_weight.reshape(sensor_rows, goal_count)
    owners = sensor_owner.reshape(sensor_rows)
    earlier = (owners[None, :] == owners[:, None]) & (row_index[None, :] < row_index[:, None])
    slot_rank = jnp.sum(earlier.astype(jnp.int32), axis=1)
    slot_index = owners * capacity + slot_rank
    placing = (
        jnp.arange(device_count * capacity, dtype=jnp.int32)[:, None] == slot_index[None, :]
    ).astype(jnp.float32)
    payload = jnp.concatenate([readings, weights], axis=1)
    outgoing = jnp.dot(placing, payload, precision=lax.Precision.HIGHEST).reshape(
        device_count, capacity, probe_count + goal_count
    )
    received = lax.all_to_all(outgoing, ("gx", "gy"), split_axis=0, concat_axis=0, tiled=True)
    goal_block = jnp.einsum(
        "scj,scp->jp",
        received[..., probe_count:],
        received[..., :probe_count],
        precision=lax.Precision.HIGHEST,
    )
    ritz_gram = lax.psum(
        jnp.dot(goal_block.T, goal_block, precision=lax.Precision.HIGHEST), ("gx", "gy")
    )
    return (state_field, goal_block, ritz_gram)


def solution(mesh):
    placed = (
        P(None, "gx", "gy", None),
        P("gx", "gy", None),
        P(),
        P("gx", "gy", None),
        P("gx", "gy", None, None),
        P("gx", "gy"),
        P("gx", "gy", None, None),
    )
    return jax.shard_map(
        body,
        mesh=mesh,
        in_specs=placed,
        out_specs=(P(None, "gx", "gy", None), P(("gx", "gy"), None), P()),
        check_vma=False,
    )
```

profile of v0, /device:TPU:0, one launch (start us, length us, event | category | flops | bytes accessed | tf_op | source)
XLA Modules:
  0.0 530.0 jit_solution(1779432885856855623)
XLA Ops:
  0.7 10.1 %copy.60 = f32[16,16,32,256]{3,0,2,1:T(8,128)S(1)} copy(f32[16,16,32,256]{3,2,1,0:T(8,128)} %param.7) | data formatting | bytes 16777216 | tf_op args[0]
  10.8 2.4 collective-permute-start.1
  13.3 1.8 collective-permute-start
  16.0 10.0 %constant_dynamic-update-slice_fusion.1 = f32[16,18,32,256]{3,0,2,1:T(8,128)} fusion(f32[16,18,32,256]{3,0,2,1:T(8,128)} %constant_dynamic-update-slice_fusion.2, f32[16,16,32,256]{3,2,1,0:T(8,128)S(1)} %copy-done), kind=kLoop, calls=%fused_computation.202 | loop fusion | bytes 16777216
  29.3 4.9 collective-permute-start.3
  34.9 2.1 multiply_add_fusion
  38.4 25.3 %fusion.81 = f32[16,16,32,256]{3,0,2,1:T(8,128)} fusion(f32[16,16,32,256]{3,0,2,1:T(8,128)} %copy-done.2, f32[16,18,32,256]{3,0,2,1:T(8,128)} %constant_dynamic-update-slice_fusion, f32[16,18,1,256]{3,0,2,1:T(8,128)S(1)} %collective-permute-done.3, f32[16,18,1,256]{3,0,2,1:T(8,128)S(1)} %collective-permute-done.2, ...), kind=kLoop, calls=%fused_computation.158 | loop fusion | flops 41943040 | bytes 29032460 | tf_op jit(solution)/shard_map/jit(_where)/select_n | solution.py:42
  66.3 7.8 %collective-permute-start.5 = (f32[16,1,32,256]{3,0,2,1:T(8,128)S(1)}, f32[16,1,32,256]{3,0,2,1:T(8,128)S(1)}, u32[]{:S(2)}, u32[]{:S(2)}) collective-permute-start(f32[16,1,32,256]{3,0,2,1:T(8,128)S(1)} %get-tuple-element.40), channel_id=1, source_target_pairs={{0,4},{4,8},{8,12},{12,16},{16,20},{20,24},{24,28},{1,5},{5,9},{9,... | collective-permute-start | bytes 1572872 | tf_op jit(solution)/shard_map/ppermute | solution.py:19
  74.1 1.5 collective-permute-done.5
  78.0 4.9 collective-permute-start.7
  82.9 2.6 collective-permute-done.6
  85.5 1.5 collective-permute-done.7
  86.9 24.8 %fusion.87 = f32[16,16,32,256]{3,0,2,1:T(8,128)} fusion(f32[16,16,32,256]{3,0,2,1:T(8,128)} %fusion.81, f32[16,1,32,256]{3,0,2,1:T(8,128)S(1)} %collective-permute-done.4, f32[16,1,32,256]{3,0,2,1:T(8,128)S(1)} %collective-permute-done.5, f32[16,18,1,256]{3,0,2,1:T(8,128)S(1)} %collective-permute-done.7, f32[16,18,1,256]{3,0,2,1:T(8,128)S(1)} %collective-permute-done.6, ...), kind=kLoop, calls=%fused_computation.164 | loop fusion | flops 50331648 | bytes 27983884 | tf_op jit(solution)/shard_map/jit(_where)/select_n | solution.py:42
  114.4 12.9 %collective-permute-start.9 = (f32[16,1,32,256]{3,0,2,1:T(8,128)S(1)}, f32[16,1,32,256]{3,0,2,1:T(8,128)S(1)}, u32[]{:S(2)}, u32[]{:S(2)}) collective-permute-start(f32[16,1,32,256]{3,0,2,1:T(8,128)S(1)} %get-tuple-element.38), channel_id=1, source_target_pairs={{0,4},{4,8},{8,12},{12,16},{16,20},{20,24},{24,28},{1,5},{5,9},{9,... | collective-permute-start | bytes 1572872 | tf_op jit(solution)/shard_map/ppermute | solution.py:19
  127.3 1.5 collective-permute-done.9
  131.2 4.7 collective-permute-start.11
  135.9 2.7 collective-permute-done.10
  140.1 24.8 %fusion.86 = f32[16,16,32,256]{3,0,2,1:T(8,128)} fusion(f32[16,16,32,256]{3,0,2,1:T(8,128)} %fusion.87, f32[16,1,32,256]{3,0,2,1:T(8,128)S(1)} %collective-permute-done.8, f32[16,1,32,256]{3,0,2,1:T(8,128)S(1)} %collective-permute-done.9, f32[16,18,1,256]{3,0,2,1:T(8,128)S(1)} %collective-permute-done.11, ...), kind=kLoop, calls=%fused_computation.163 | loop fusion | flops 50331648 | bytes 27983884 | tf_op jit(solution)/shard_map/jit(_where)/select_n | solution.py:42
  167.4 10.1 %collective-permute-start.13 = (f32[16,1,32,256]{3,0,2,1:T(8,128)S(1)}, f32[16,1,32,256]{3,0,2,1:T(8,128)S(1)}, u32[]{:S(2)}, u32[]{:S(2)}) collective-permute-start(f32[16,1,32,256]{3,0,2,1:T(8,128)S(1)} %get-tuple-element.36), channel_id=1, source_target_pairs={{0,4},{4,8},{8,12},{12,16},{16,20},{20,24},{24,28},{1,5},{5,9},{9,... | collective-permute-start | bytes 1572872 | tf_op jit(solution)/shard_map/ppermute | solution.py:19
  177.6 1.5 collective-permute-done.13
  181.4 4.8 collective-permute-start.15
  186.3 2.7 collective-permute-done.14
  189.0 1.5 collective-permute-done.15
  190.5 24.2 %fusion.85 = f32[16,16,32,256]{3,0,2,1:T(8,128)S(1)} fusion(f32[16,16,32,256]{3,0,2,1:T(8,128)} %fusion.86, f32[16,1,32,256]{3,0,2,1:T(8,128)S(1)} %collective-permute-done.12, f32[16,1,32,256]{3,0,2,1:T(8,128)S(1)} %collective-permute-done.13, f32[16,18,1,256]{3,0,2,1:T(8,128)S(1)} %collective-permute-done.15, ...), kind=kLoop, calls=%fused_computation.162 | loop fusion | flops 50331648 | bytes 27983884 | tf_op jit(solution)/shard_map/jit(_where)/select_n | solution.py:42
  216.1 9.8 %collective-permute-start.17 = (f32[16,1,32,256]{3,0,2,1:T(8,128)S(1)}, f32[16,1,32,256]{3,0,2,1:T(8,128)S(1)}, u32[]{:S(2)}, u32[]{:S(2)}) collective-permute-start(f32[16,1,32,256]{3,0,2,1:T(8,128)S(1)} %get-tuple-element.34), channel_id=1, source_target_pairs={{0,4},{4,8},{8,12},{12,16},{16,20},{20,24},{24,28},{1,5},{5,9},{9,... | collective-permute-start | bytes 1572872 | tf_op jit(solution)/shard_map/ppermute | solution.py:19
  225.9 1.5 collective-permute-done.17
  228.7 5.1 collective-permute-start.19
  233.8 2.5 collective-permute-done.18
  237.8 13.1 %fusion.80 = f32[16,16,32,256]{3,0,2,1:T(8,128)} fusion(f32[16,16,32,256]{3,0,2,1:T(8,128)S(1)} %fusion.85, f32[16,1,32,256]{3,0,2,1:T(8,128)S(1)} %collective-permute-done.16, f32[16,1,32,256]{3,0,2,1:T(8,128)S(1)} %collective-permute-done.17, f32[16,18,1,256]{3,0,2,1:T(8,128)S(1)} %collective-permute-done.19, ...), kind=kLoop, calls=%fused_computation.157 | loop fusion | flops 50331648 | bytes 19595276 | tf_op jit(solution)/shard_map/jit(_where)/select_n | solution.py:42
  253.5 9.8 %collective-permute-start.21 = (f32[16,1,32,256]{3,0,2,1:T(8,128)S(1)}, f32[16,1,32,256]{3,0,2,1:T(8,128)S(1)}, u32[]{:S(2)}, u32[]{:S(2)}) collective-permute-start(f32[16,1,32,256]{3,0,2,1:T(8,128)S(1)} %get-tuple-element.32), channel_id=1, source_target_pairs={{0,4},{4,8},{8,12},{12,16},{16,20},{20,24},{24,28},{1,5},{5,9},{9,... | collective-permute-start | bytes 1572872 | tf_op jit(solution)/shard_map/ppermute | solution.py:19
  263.3 1.5 collective-permute-done.21
  267.1 4.8 collective-permute-start.23
  272.0 2.7 collective-permute-done.22
  276.2 22.7 %fusion.84 = f32[16,16,32,256]{3,0,2,1:T(8,128)} fusion(f32[16,16,32,256]{3,0,2,1:T(8,128)S(1)} %fusion.85, f32[16,16,32,256]{3,0,2,1:T(8,128)} %fusion.80, f32[16,1,32,256]{3,0,2,1:T(8,128)S(1)} %collective-permute-done.20, f32[16,1,32,256]{3,0,2,1:T(8,128)S(1)} %collective-permute-done.21, f32[16,18,1,256]{3,0,2,1:T(8,128)S(1)} %collective-permute-done.23, ...), kind=kLoop, calls=%fused_computation.161 | loop fusion | flops 50331648 | bytes 27983884 | tf_op jit(solution)/shard_map/jit(_where)/select_n | solution.py:42
  301.5 11.3 %collective-permute-start.25 = (f32[16,1,32,256]{3,0,2,1:T(8,128)S(1)}, f32[16,1,32,256]{3,0,2,1:T(8,128)S(1)}, u32[]{:S(2)}, u32[]{:S(2)}) collective-permute-start(f32[16,1,32,256]{3,0,2,1:T(8,128)S(1)} %get-tuple-element.30), channel_id=1, source_target_pairs={{0,4},{4,8},{8,12},{12,16},{16,20},{20,24},{24,28},{1,5},{5,9},{9,... | collective-permute-start | bytes 1572872 | tf_op jit(solution)/shard_map/ppermute | solution.py:19
  312.8 1.5 collective-permute-done.25
  316.7 4.7 collective-permute-start.27
  322.1 2.1 collective-permute-done.26
  325.6 22.7 %fusion.83 = f32[16,16,32,256]{3,0,2,1:T(8,128)} fusion(f32[16,16,32,256]{3,0,2,1:T(8,128)S(1)} %fusion.85, f32[16,16,32,256]{3,0,2,1:T(8,128)} %fusion.84, f32[16,1,32,256]{3,0,2,1:T(8,128)S(1)} %collective-permute-done.24, f32[16,1,32,256]{3,0,2,1:T(8,128)S(1)} %collective-permute-done.25, f32[16,18,1,256]{3,0,2,1:T(8,128)S(1)} %collective-permute-done.27, ...), kind=kLoop, calls=%fused_computation.160 | loop fusion | flops 50331648 | bytes 27983884 | tf_op jit(solution)/shard_map/jit(_where)/select_n | solution.py:42
  350.9 13.9 %collective-permute-start.29 = (f32[16,1,32,256]{3,0,2,1:T(8,128)S(1)}, f32[16,1,32,256]{3,0,2,1:T(8,128)S(1)}, u32[]{:S(2)}, u32[]{:S(2)}) collective-permute-start(f32[16,1,32,256]{3,0,2,1:T(8,128)S(1)} %get-tuple-element.28), channel_id=1, source_target_pairs={{0,4},{4,8},{8,12},{12,16},{16,20},{20,24},{24,28},{1,5},{5,9},{9,... | collective-permute-start | bytes 1572872 | tf_op jit(solution)/shard_map/ppermute | solution.py:19
  368.7 4.7 collective-permute-start.31
  373.5 2.7 collective-permute-done.30
  377.7 22.7 %fusion.82 = f32[16,16,32,256]{3,0,2,1:T(8,128)} fusion(f32[16,16,32,256]{3,0,2,1:T(8,128)S(1)} %fusion.85, f32[16,16,32,256]{3,0,2,1:T(8,128)} %fusion.83, f32[16,1,32,256]{3,0,2,1:T(8,128)S(1)} %collective-permute-done.28, f32[16,1,32,256]{3,0,2,1:T(8,128)S(1)} %collective-permute-done.29, f32[16,18,1,256]{3,0,2,1:T(8,128)S(1)} %collective-permute-done.31, ...), kind=kLoop, calls=%fused_computation.159 | loop fusion | flops 50331648 | bytes 27983884 | tf_op jit(solution)/shard_map/jit(_where)/select_n | solution.py:42
  400.4 32.9 %copy.61 = f32[16,16,32,256]{0,3,2,1:T(8,128)} copy(f32[16,16,32,256]{3,0,2,1:T(8,128)} %fusion.82) | data formatting | bytes 16777216 | tf_op jit(solution)/shard_map/jit(_where)/select_n | solution.py:42
  433.3 1.8 gather_fusion
  436.0 39.7 %all-to-all-start = ((f32[32,1,128]{2,1,0:T(1,128)}), f32[32,1,128]{2,1,0:T(1,128)S(1)}, u32[]{:S(2)}, u32[]{:S(2)}) async-start(f32[32,1,128]{2,1,0:T(1,128)} %reshape.93), calls=%async_computation | async-start | bytes 32768 | tf_op jit(solution)/shard_map/all_to_all | solution.py:74
  475.7 11.6 %copy.66 = f32[16,16,32,256]{3,2,1,0:T(8,128)} copy(f32[16,16,32,256]{3,0,2,1:T(8,128)} %fusion.82) | data formatting | bytes 16777216
  489.2 40.6 %psum.7 = f32[16,16]{1,0:T(8,128)} all-reduce(f32[16,16]{1,0:T(8,128)S(1)} %fusion.109), channel_id=1, replica_groups=mesh['gx'=8,'gy'=4] {'gx','gy'}, use_global_device_ids=true, to_apply=%region_1.2 | all-reduce | flops 256 | bytes 2048 | tf_op jit(solution)/shard_map/psum | solution.py:81
  (84 shorter events, 50.1 us)
Async XLA Ops:
  0.6 15.4 %copy-start = (f32[16,16,32,256]{3,2,1,0:T(8,128)S(1)}, f32[16,16,32,256]{3,2,1,0:T(8,128)}, u32[]{:S(2)}) copy-start(f32[16,16,32,256]{3,2,1,0:T(8,128)} %param.7) | copy-start | bytes 25165828
  0.6 14.4 %copy-start.1 = (f32[16,32,256]{2,1,0:T(8,128)S(1)}, f32[16,32,256]{2,1,0:T(8,128)}, u32[]{:S(2)}) copy-start(f32[16,32,256]{2,1,0:T(8,128)} %param.8) | copy-start | bytes 1572868
  10.7 15.3 %copy-start.2 = (f32[16,16,32,256]{3,0,2,1:T(8,128)}, f32[16,16,32,256]{3,0,2,1:T(8,128)S(1)}, u32[]{:S(2)}) copy-start(f32[16,16,32,256]{3,0,2,1:T(8,128)S(1)} %copy.60) | copy-start | bytes 25165828
  10.8 4.4 collective-permute-start.1
  13.3 12.8 %collective-permute-start = (f32[16,1,32,256]{3,0,2,1:T(8,128)S(1)}, f32[16,1,32,256]{3,0,2,1:T(8,128)S(1)}, u32[]{:S(2)}, u32[]{:S(2)}) collective-permute-start(f32[16,1,32,256]{3,0,2,1:T(8,128)S(1)} %get-tuple-element.42), channel_id=1, source_target_pairs={{4,0},{8,4},{12,8},{16,12},{20,16},{24,20},{28,24},{5,1},{9,5},{13... | collective-permute-start | bytes 1572872 | tf_op jit(solution)/shard_map/ppermute | solution.py:21
  16.0 18.2 %copy-start.5 = (f32[3]{0:T(128)S(1)}, f32[3]{0:T(128)}, u32[]{:S(2)}) copy-start(f32[3]{0:T(128)} %param.9) | copy-start | bytes 40
  28.0 9.0 %collective-permute-start.2 = (f32[16,18,1,256]{3,0,2,1:T(8,128)S(1)}, f32[16,18,1,256]{3,0,2,1:T(8,128)S(1)}, u32[]{:S(2)}, u32[]{:S(2)}) collective-permute-start(f32[16,18,1,256]{3,0,2,1:T(8,128)S(1)} %get-tuple-element.26), channel_id=1, source_target_pairs={{1,0},{2,1},{3,2},{5,4},{6,5},{7,6},{9,8},{10,9},{11,10},{13,12},{... | collective-permute-start | bytes 884744 | tf_op jit(solution)/shard_map/ppermute | solution.py:21
  29.3 9.2 %collective-permute-start.3 = (f32[16,18,1,256]{3,0,2,1:T(8,128)S(1)}, f32[16,18,1,256]{3,0,2,1:T(8,128)S(1)}, u32[]{:S(2)}, u32[]{:S(2)}) collective-permute-start(f32[16,18,1,256]{3,0,2,1:T(8,128)S(1)} %get-tuple-element.27), channel_id=1, source_target_pairs={{0,1},{1,2},{2,3},{4,5},{5,6},{6,7},{8,9},{9,10},{10,11},{12,13},{... | collective-permute-start | bytes 884744 | tf_op jit(solution)/shard_map/ppermute | solution.py:19
  65.0 9.1 %collective-permute-start.4 = (f32[16,1,32,256]{3,0,2,1:T(8,128)S(1)}, f32[16,1,32,256]{3,0,2,1:T(8,128)S(1)}, u32[]{:S(2)}, u32[]{:S(2)}) collective-permute-start(f32[16,1,32,256]{3,0,2,1:T(8,128)S(1)} %get-tuple-element.41), channel_id=1, source_target_pairs={{4,0},{8,4},{12,8},{16,12},{20,16},{24,20},{28,24},{5,1},{9,5},{13... | collective-permute-start | bytes 1572872 | tf_op jit(solution)/shard_map/ppermute | solution.py:21
  66.3 9.3 %collective-permute-start.5 = (f32[16,1,32,256]{3,0,2,1:T(8,128)S(1)}, f32[16,1,32,256]{3,0,2,1:T(8,128)S(1)}, u32[]{:S(2)}, u32[]{:S(2)}) collective-permute-start(f32[16,1,32,256]{3,0,2,1:T(8,128)S(1)} %get-tuple-element.40), channel_id=1, source_target_pairs={{0,4},{4,8},{8,12},{12,16},{16,20},{20,24},{24,28},{1,5},{5,9},{9,... | collective-permute-start | bytes 1572872 | tf_op jit(solution)/shard_map/ppermute | solution.py:19
  76.7 8.8 %collective-permute-start.6 = (f32[16,18,1,256]{3,0,2,1:T(8,128)S(1)}, f32[16,18,1,256]{3,0,2,1:T(8,128)S(1)}, u32[]{:S(2)}, u32[]{:S(2)}) collective-permute-start(f32[16,18,1,256]{3,0,2,1:T(8,128)S(1)} %get-tuple-element.24), channel_id=1, source_target_pairs={{1,0},{2,1},{3,2},{5,4},{6,5},{7,6},{9,8},{10,9},{11,10},{13,12},{... | collective-permute-start | bytes 884744 | tf_op jit(solution)/shard_map/ppermute | solution.py:21
  78.0 8.9 %collective-permute-start.7 = (f32[16,18,1,256]{3,0,2,1:T(8,128)S(1)}, f32[16,18,1,256]{3,0,2,1:T(8,128)S(1)}, u32[]{:S(2)}, u32[]{:S(2)}) collective-permute-start(f32[16,18,1,256]{3,0,2,1:T(8,128)S(1)} %get-tuple-element.25), channel_id=1, source_target_pairs={{0,1},{1,2},{2,3},{4,5},{5,6},{6,7},{8,9},{9,10},{10,11},{12,13},{... | collective-permute-start | bytes 884744 | tf_op jit(solution)/shard_map/ppermute | solution.py:19
  113.1 14.2 %collective-permute-start.8 = (f32[16,1,32,256]{3,0,2,1:T(8,128)S(1)}, f32[16,1,32,256]{3,0,2,1:T(8,128)S(1)}, u32[]{:S(2)}, u32[]{:S(2)}) collective-permute-start(f32[16,1,32,256]{3,0,2,1:T(8,128)S(1)} %get-tuple-element.39), channel_id=1, source_target_pairs={{4,0},{8,4},{12,8},{16,12},{20,16},{24,20},{28,24},{5,1},{9,5},{13... | collective-permute-start | bytes 1572872 | tf_op jit(solution)/shard_map/ppermute | solution.py:21
  114.4 14.4 %collective-permute-start.9 = (f32[16,1,32,256]{3,0,2,1:T(8,128)S(1)}, f32[16,1,32,256]{3,0,2,1:T(8,128)S(1)}, u32[]{:S(2)}, u32[]{:S(2)}) collective-permute-start(f32[16,1,32,256]{3,0,2,1:T(8,128)S(1)} %get-tuple-element.38), channel_id=1, source_target_pairs={{0,4},{4,8},{8,12},{12,16},{16,20},{20,24},{24,28},{1,5},{5,9},{9,... | collective-permute-start | bytes 1572872 | tf_op jit(solution)/shard_map/ppermute | solution.py:19
  129.9 8.8 %collective-permute-start.10 = (f32[16,18,1,256]{3,0,2,1:T(8,128)S(1)}, f32[16,18,1,256]{3,0,2,1:T(8,128)S(1)}, u32[]{:S(2)}, u32[]{:S(2)}) collective-permute-start(f32[16,18,1,256]{3,0,2,1:T(8,128)S(1)} %get-tuple-element.22), channel_id=1, source_target_pairs={{1,0},{2,1},{3,2},{5,4},{6,5},{7,6},{9,8},{10,9},{11,10},{13,12},{... | collective-permute-start | bytes 884744 | tf_op jit(solution)/shard_map/ppermute | solution.py:21
  131.2 8.9 %collective-permute-start.11 = (f32[16,18,1,256]{3,0,2,1:T(8,128)S(1)}, f32[16,18,1,256]{3,0,2,1:T(8,128)S(1)}, u32[]{:S(2)}, u32[]{:S(2)}) collective-permute-start(f32[16,18,1,256]{3,0,2,1:T(8,128)S(1)} %get-tuple-element.23), channel_id=1, source_target_pairs={{0,1},{1,2},{2,3},{4,5},{5,6},{6,7},{8,9},{9,10},{10,11},{12,13},{... | collective-permute-start | bytes 884744 | tf_op jit(solution)/shard_map/ppermute | solution.py:19
  166.1 11.4 %collective-permute-start.12 = (f32[16,1,32,256]{3,0,2,1:T(8,128)S(1)}, f32[16,1,32,256]{3,0,2,1:T(8,128)S(1)}, u32[]{:S(2)}, u32[]{:S(2)}) collective-permute-start(f32[16,1,32,256]{3,0,2,1:T(8,128)S(1)} %get-tuple-element.37), channel_id=1, source_target_pairs={{4,0},{8,4},{12,8},{16,12},{20,16},{24,20},{28,24},{5,1},{9,5},{13... | collective-permute-start | bytes 1572872 | tf_op jit(solution)/shard_map/ppermute | solution.py:21
  167.4 11.6 %collective-permute-start.13 = (f32[16,1,32,256]{3,0,2,1:T(8,128)S(1)}, f32[16,1,32,256]{3,0,2,1:T(8,128)S(1)}, u32[]{:S(2)}, u32[]{:S(2)}) collective-permute-start(f32[16,1,32,256]{3,0,2,1:T(8,128)S(1)} %get-tuple-element.36), channel_id=1, source_target_pairs={{0,4},{4,8},{8,12},{12,16},{16,20},{20,24},{24,28},{1,5},{5,9},{9,... | collective-permute-start | bytes 1572872 | tf_op jit(solution)/shard_map/ppermute | solution.py:19
  180.1 8.9 %collective-permute-start.14 = (f32[16,18,1,256]{3,0,2,1:T(8,128)S(1)}, f32[16,18,1,256]{3,0,2,1:T(8,128)S(1)}, u32[]{:S(2)}, u32[]{:S(2)}) collective-permute-start(f32[16,18,1,256]{3,0,2,1:T(8,128)S(1)} %get-tuple-element.20), channel_id=1, source_target_pairs={{1,0},{2,1},{3,2},{5,4},{6,5},{7,6},{9,8},{10,9},{11,10},{13,12},{... | collective-permute-start | bytes 884744 | tf_op jit(solution)/shard_map/ppermute | solution.py:21
  181.4 9.1 %collective-permute-start.15 = (f32[16,18,1,256]{3,0,2,1:T(8,128)S(1)}, f32[16,18,1,256]{3,0,2,1:T(8,128)S(1)}, u32[]{:S(2)}, u32[]{:S(2)}) collective-permute-start(f32[16,18,1,256]{3,0,2,1:T(8,128)S(1)} %get-tuple-element.21), channel_id=1, source_target_pairs={{0,1},{1,2},{2,3},{4,5},{5,6},{6,7},{8,9},{9,10},{10,11},{12,13},{... | collective-permute-start | bytes 884744 | tf_op jit(solution)/shard_map/ppermute | solution.py:19
  214.8 11.1 %collective-permute-start.16 = (f32[16,1,32,256]{3,0,2,1:T(8,128)S(1)}, f32[16,1,32,256]{3,0,2,1:T(8,128)S(1)}, u32[]{:S(2)}, u32[]{:S(2)}) collective-permute-start(f32[16,1,32,256]{3,0,2,1:T(8,128)S(1)} %get-tuple-element.35), channel_id=1, source_target_pairs={{4,0},{8,4},{12,8},{16,12},{20,16},{24,20},{28,24},{5,1},{9,5},{13... | collective-permute-start | bytes 1572872 | tf_op jit(solution)/shard_map/ppermute | solution.py:21
  216.1 11.3 %collective-permute-start.17 = (f32[16,1,32,256]{3,0,2,1:T(8,128)S(1)}, f32[16,1,32,256]{3,0,2,1:T(8,128)S(1)}, u32[]{:S(2)}, u32[]{:S(2)}) collective-permute-start(f32[16,1,32,256]{3,0,2,1:T(8,128)S(1)} %get-tuple-element.34), channel_id=1, source_target_pairs={{0,4},{4,8},{8,12},{12,16},{16,20},{20,24},{24,28},{1,5},{5,9},{9,... | collective-permute-start | bytes 1572872 | tf_op jit(solution)/shard_map/ppermute | solution.py:19
  227.4 8.9 %collective-permute-start.18 = (f32[16,18,1,256]{3,0,2,1:T(8,128)S(1)}, f32[16,18,1,256]{3,0,2,1:T(8,128)S(1)}, u32[]{:S(2)}, u32[]{:S(2)}) collective-permute-start(f32[16,18,1,256]{3,0,2,1:T(8,128)S(1)} %get-tuple-element.18), channel_id=1, source_target_pairs={{1,0},{2,1},{3,2},{5,4},{6,5},{7,6},{9,8},{10,9},{11,10},{13,12},{... | collective-permute-start | bytes 884744 | tf_op jit(solution)/shard_map/ppermute | solution.py:21
  228.7 9.1 %collective-permute-start.19 = (f32[16,18,1,256]{3,0,2,1:T(8,128)S(1)}, f32[16,18,1,256]{3,0,2,1:T(8,128)S(1)}, u32[]{:S(2)}, u32[]{:S(2)}) collective-permute-start(f32[16,18,1,256]{3,0,2,1:T(8,128)S(1)} %get-tuple-element.19), channel_id=1, source_target_pairs={{0,1},{1,2},{2,3},{4,5},{5,6},{6,7},{8,9},{9,10},{10,11},{12,13},{... | collective-permute-start | bytes 884744 | tf_op jit(solution)/shard_map/ppermute | solution.py:19
  252.2 11.1 %collective-permute-start.20 = (f32[16,1,32,256]{3,0,2,1:T(8,128)S(1)}, f32[16,1,32,256]{3,0,2,1:T(8,128)S(1)}, u32[]{:S(2)}, u32[]{:S(2)}) collective-permute-start(f32[16,1,32,256]{3,0,2,1:T(8,128)S(1)} %get-tuple-element.33), channel_id=1, source_target_pairs={{4,0},{8,4},{12,8},{16,12},{20,16},{24,20},{28,24},{5,1},{9,5},{13... | collective-permute-start | bytes 1572872 | tf_op jit(solution)/shard_map/ppermute | solution.py:21
  253.5 11.3 %collective-permute-start.21 = (f32[16,1,32,256]{3,0,2,1:T(8,128)S(1)}, f32[16,1,32,256]{3,0,2,1:T(8,128)S(1)}, u32[]{:S(2)}, u32[]{:S(2)}) collective-permute-start(f32[16,1,32,256]{3,0,2,1:T(8,128)S(1)} %get-tuple-element.32), channel_id=1, source_target_pairs={{0,4},{4,8},{8,12},{12,16},{16,20},{20,24},{24,28},{1,5},{5,9},{9,... | collective-permute-start | bytes 1572872 | tf_op jit(solution)/shard_map/ppermute | solution.py:19
  265.8 8.9 %collective-permute-start.22 = (f32[16,18,1,256]{3,0,2,1:T(8,128)S(1)}, f32[16,18,1,256]{3,0,2,1:T(8,128)S(1)}, u32[]{:S(2)}, u32[]{:S(2)}) collective-permute-start(f32[16,18,1,256]{3,0,2,1:T(8,128)S(1)} %get-tuple-element.16), channel_id=1, source_target_pairs={{1,0},{2,1},{3,2},{5,4},{6,5},{7,6},{9,8},{10,9},{11,10},{13,12},{... | collective-permute-start | bytes 884744 | tf_op jit(solution)/shard_map/ppermute | solution.py:21
  267.1 9.1 %collective-permute-start.23 = (f32[16,18,1,256]{3,0,2,1:T(8,128)S(1)}, f32[16,18,1,256]{3,0,2,1:T(8,128)S(1)}, u32[]{:S(2)}, u32[]{:S(2)}) collective-permute-start(f32[16,18,1,256]{3,0,2,1:T(8,128)S(1)} %get-tuple-element.17), channel_id=1, source_target_pairs={{0,1},{1,2},{2,3},{4,5},{5,6},{6,7},{8,9},{9,10},{10,11},{12,13},{... | collective-permute-start | bytes 884744 | tf_op jit(solution)/shard_map/ppermute | solution.py:19
  300.2 12.6 %collective-permute-start.24 = (f32[16,1,32,256]{3,0,2,1:T(8,128)S(1)}, f32[16,1,32,256]{3,0,2,1:T(8,128)S(1)}, u32[]{:S(2)}, u32[]{:S(2)}) collective-permute-start(f32[16,1,32,256]{3,0,2,1:T(8,128)S(1)} %get-tuple-element.31), channel_id=1, source_target_pairs={{4,0},{8,4},{12,8},{16,12},{20,16},{24,20},{28,24},{5,1},{9,5},{13... | collective-permute-start | bytes 1572872 | tf_op jit(solution)/shard_map/ppermute | solution.py:21
  301.5 12.8 %collective-permute-start.25 = (f32[16,1,32,256]{3,0,2,1:T(8,128)S(1)}, f32[16,1,32,256]{3,0,2,1:T(8,128)S(1)}, u32[]{:S(2)}, u32[]{:S(2)}) collective-permute-start(f32[16,1,32,256]{3,0,2,1:T(8,128)S(1)} %get-tuple-element.30), channel_id=1, source_target_pairs={{0,4},{4,8},{8,12},{12,16},{16,20},{20,24},{24,28},{1,5},{5,9},{9,... | collective-permute-start | bytes 1572872 | tf_op jit(solution)/shard_map/ppermute | solution.py:19
  315.4 8.8 %collective-permute-start.26 = (f32[16,18,1,256]{3,0,2,1:T(8,128)S(1)}, f32[16,18,1,256]{3,0,2,1:T(8,128)S(1)}, u32[]{:S(2)}, u32[]{:S(2)}) collective-permute-start(f32[16,18,1,256]{3,0,2,1:T(8,128)S(1)} %get-tuple-element.14), channel_id=1, source_target_pairs={{1,0},{2,1},{3,2},{5,4},{6,5},{7,6},{9,8},{10,9},{11,10},{13,12},{... | collective-permute-start | bytes 884744 | tf_op jit(solution)/shard_map/ppermute | solution.py:21
  316.7 8.9 %collective-permute-start.27 = (f32[16,18,1,256]{3,0,2,1:T(8,128)S(1)}, f32[16,18,1,256]{3,0,2,1:T(8,128)S(1)}, u32[]{:S(2)}, u32[]{:S(2)}) collective-permute-start(f32[16,18,1,256]{3,0,2,1:T(8,128)S(1)} %get-tuple-element.15), channel_id=1, source_target_pairs={{0,1},{1,2},{2,3},{4,5},{5,6},{6,7},{8,9},{9,10},{10,11},{12,13},{... | collective-permute-start | bytes 884744 | tf_op jit(solution)/shard_map/ppermute | solution.py:19
  322.1 42.8 %copy-start.7 = (s32[1,1,128,1]{2,3,1,0:T(1,128)S(1)}, s32[1,1,128,1]{2,3,1,0:T(1,128)}, u32[]{:S(2)}) copy-start(s32[1,1,128,1]{2,3,1,0:T(1,128)} %param.11) | copy-start | bytes 1540
  322.1 43.0 %copy-start.6 = (s32[1,1,128]{2,1,0:T(1,128)S(1)}, s32[1,1,128]{2,1,0:T(1,128)}, u32[]{:S(2)}) copy-start(s32[1,1,128]{2,1,0:T(1,128)} %param.10) | copy-start | bytes 1540
  349.6 15.5 %collective-permute-start.28 = (f32[16,1,32,256]{3,0,2,1:T(8,128)S(1)}, f32[16,1,32,256]{3,0,2,1:T(8,128)S(1)}, u32[]{:S(2)}, u32[]{:S(2)}) collective-permute-start(f32[16,1,32,256]{3,0,2,1:T(8,128)S(1)} %get-tuple-element.29), channel_id=1, source_target_pairs={{4,0},{8,4},{12,8},{16,12},{20,16},{24,20},{28,24},{5,1},{9,5},{13... | collective-permute-start | bytes 1572872 | tf_op jit(solution)/shard_map/ppermute | solution.py:21
  350.9 15.4 %collective-permute-start.29 = (f32[16,1,32,256]{3,0,2,1:T(8,128)S(1)}, f32[16,1,32,256]{3,0,2,1:T(8,128)S(1)}, u32[]{:S(2)}, u32[]{:S(2)}) collective-permute-start(f32[16,1,32,256]{3,0,2,1:T(8,128)S(1)} %get-tuple-element.28), channel_id=1, source_target_pairs={{0,4},{4,8},{8,12},{12,16},{16,20},{20,24},{24,28},{1,5},{5,9},{9,... | collective-permute-start | bytes 1572872 | tf_op jit(solution)/shard_map/ppermute | solution.py:19
  367.4 8.8 %collective-permute-start.30 = (f32[16,18,1,256]{3,0,2,1:T(8,128)S(1)}, f32[16,18,1,256]{3,0,2,1:T(8,128)S(1)}, u32[]{:S(2)}, u32[]{:S(2)}) collective-permute-start(f32[16,18,1,256]{3,0,2,1:T(8,128)S(1)} %get-tuple-element.12), channel_id=1, source_target_pairs={{1,0},{2,1},{3,2},{5,4},{6,5},{7,6},{9,8},{10,9},{11,10},{13,12},{... | collective-permute-start | bytes 884744 | tf_op jit(solution)/shard_map/ppermute | solution.py:21
  368.7 8.9 %collective-permute-start.31 = (f32[16,18,1,256]{3,0,2,1:T(8,128)S(1)}, f32[16,18,1,256]{3,0,2,1:T(8,128)S(1)}, u32[]{:S(2)}, u32[]{:S(2)}) collective-permute-start(f32[16,18,1,256]{3,0,2,1:T(8,128)S(1)} %get-tuple-element.13), channel_id=1, source_target_pairs={{0,1},{1,2},{2,3},{4,5},{5,6},{6,7},{8,9},{9,10},{10,11},{12,13},{... | collective-permute-start | bytes 884744 | tf_op jit(solution)/shard_map/ppermute | solution.py:19
  400.4 34.7 %copy-start.4 = (f32[1,1,128,16]{2,3,1,0:T(8,128)S(1)}, f32[1,1,128,16]{2,3,1,0:T(8,128)}, u32[]{:S(2)}) copy-start(f32[1,1,128,16]{2,3,1,0:T(8,128)} %param.13) | copy-start | bytes 24580
  436.0 51.3 %all-to-all-start = ((f32[32,1,128]{2,1,0:T(1,128)}), f32[32,1,128]{2,1,0:T(1,128)S(1)}, u32[]{:S(2)}, u32[]{:S(2)}) async-start(f32[32,1,128]{2,1,0:T(1,128)} %reshape.93), calls=%async_computation | async-start | bytes 32768 | tf_op jit(solution)/shard_map/all_to_all | solution.py:74
  488.9 40.8 %copy-start.3 = (f32[16,16]{1,0:T(8,128)}, f32[16,16]{1,0:T(8,128)S(1)}, u32[]{:S(2)}) copy-start(f32[16,16]{1,0:T(8,128)S(1)} %convolution_bitcast_fusion) | copy-start | bytes 3076
where the time goes:
time: 538 us; the launch traced here: 530 us
  other arithmetic  190 us (35%)
  starting transfers between devices  178 us (33%)
  local copies, waits for them, and re-layouts  79 us (15%)
  blocking collectives  40.6 us (8%)
  waiting for transfers between devices  39.9 us (7%)
    select_n x8, other arithmetic, relax(): return jnp.where(diffusion > 0.0, updated, 0.0)  180 us
    ppermute x16, starting transfers between devices, padded_2(): lax.ppermute(tail, axis, [(i, (i + 1) % count) for i in range(ends)])  117 us
    psum x1, blocking collectives, body(): lax.psum(jnp.dot(goal_block.T, goal_block, precision=lax.Precision.HIGHES...  40.6 us
    all_to_all x1, starting transfers between devices, body(): lax.all_to_all(outgoing, ('gx', 'gy'), split_axis=0, concat_axis=0, tiled...  39.7 us
    unnamed x22, local copies, waits for them, and re-layouts  33.4 us
    select_n x1, local copies, waits for them, and re-layouts, relax(): return jnp.where(diffusion > 0.0, updated, 0.0)  32.9 us
    ppermute x16, waiting for transfers between devices, padded_2(): lax.ppermute(tail, axis, [(i, (i + 1) % count) for i in range(ends)])  21.8 us
    ppermute x16, starting transfers between devices, padded_2(): lax.ppermute(head, axis, [((i + 1) % count, i) for i in range(ends)])  21.2 us
  transfers between devices with their start and end apart: 33, of which 22 were waited for; matrix products, arithmetic and copies ran while one was open for 5% of the time, Pallas kernels for 0%

commit v1 on v0

--- a/solution.py
+++ b/solution.py
@@ -78,9 +78,8 @@
         received[..., :probe_count],
         precision=lax.Precision.HIGHEST,
     )
-    ritz_gram = lax.psum(
-        jnp.dot(goal_block.T, goal_block, precision=lax.Precision.HIGHEST), ("gx", "gy")
-    )
+    inner = lax.psum(jnp.dot(goal_block.T, goal_block, precision=lax.Precision.HIGHEST), "gy")
+    ritz_gram = lax.psum(inner, "gx")
     return (state_field, goal_block, ritz_gram)
 
 

time: 538 us -> 522 us (0.970)
  blocking collectives: 40.6 us -> 25 us
    psum x1, blocking collectives: 40.6 us -> 12.2 us  [body(): lax.psum(jnp.dot(goal_block.T, goal_block, precision=lax.Precision.HIGHES...]
    psum x0 -> x1, blocking collectives: none -> 12.7 us  [body(): ritz_gram = lax.psum(inner, 'gx')]
  transfers between devices with their start and end apart: 33 -> 33, of which waited for: 22 -> 23; matrix products, arithmetic and copies ran while one was open for 5% -> 5% of each run, Pallas kernels for 0% -> 0%
where the time goes in v1:
time: 522 us; the launch traced here: 514 us
  other arithmetic  189 us (36%)
  starting transfers between devices  178 us (34%)
  local copies, waits for them, and re-layouts  79 us (15%)
  waiting for transfers between devices  40 us (8%)
  blocking collectives  25 us (5%)
    select_n x8, other arithmetic, relax(): return jnp.where(diffusion > 0.0, updated, 0.0)  180 us
    ppermute x16, starting transfers between devices, padded_2(): lax.ppermute(tail, axis, [(i, (i + 1) % count) for i in range(ends)])  117 us
    all_to_all x1, starting transfers between devices, body(): lax.all_to_all(outgoing, ('gx', 'gy'), split_axis=0, concat_axis=0, tiled...  39.7 us
    unnamed x22, local copies, waits for them, and re-layouts  33.4 us
    select_n x1, local copies, waits for them, and re-layouts, relax(): return jnp.where(diffusion > 0.0, updated, 0.0)  32.9 us
    ppermute x16, waiting for transfers between devices, padded_2(): lax.ppermute(tail, axis, [(i, (i + 1) % count) for i in range(ends)])  21.8 us
    ppermute x16, starting transfers between devices, padded_2(): lax.ppermute(head, axis, [((i + 1) % count, i) for i in range(ends)])  21.2 us
    ppermute x16, waiting for transfers between devices, padded_2(): lax.ppermute(head, axis, [((i + 1) % count, i) for i in range(ends)])  18.2 us
  transfers between devices with their start and end apart: 33, of which 23 were waited for; matrix products, arithmetic and copies ran while one was open for 5% of the time, Pallas kernels for 0%

profile of v1, /device:TPU:0, one launch (start us, length us, event | category | flops | bytes accessed | tf_op | source)
XLA Modules:
  0.0 513.9 jit_solution(16442050574768679717)
XLA Ops:
  0.7 10.1 %copy.60 = f32[16,16,32,256]{3,0,2,1:T(8,128)S(1)} copy(f32[16,16,32,256]{3,2,1,0:T(8,128)} %param.7) | data formatting | bytes 16777216 | tf_op args[0]
  10.8 2.4 collective-permute-start.1
  13.3 1.8 collective-permute-start
  16.0 10.0 %constant_dynamic-update-slice_fusion.1 = f32[16,18,32,256]{3,0,2,1:T(8,128)} fusion(f32[16,18,32,256]{3,0,2,1:T(8,128)} %constant_dynamic-update-slice_fusion.2, f32[16,16,32,256]{3,2,1,0:T(8,128)S(1)} %copy-done), kind=kLoop, calls=%fused_computation.202 | loop fusion | bytes 16777216
  29.3 4.9 collective-permute-start.3
  34.8 2.0 multiply_add_fusion
  37.0 1.5 collective-permute-done.3
  38.4 25.3 %fusion.81 = f32[16,16,32,256]{3,0,2,1:T(8,128)} fusion(f32[16,16,32,256]{3,0,2,1:T(8,128)} %copy-done.2, f32[16,18,32,256]{3,0,2,1:T(8,128)} %constant_dynamic-update-slice_fusion, f32[16,18,1,256]{3,0,2,1:T(8,128)S(1)} %collective-permute-done.3, f32[16,18,1,256]{3,0,2,1:T(8,128)S(1)} %collective-permute-done.2, ...), kind=kLoop, calls=%fused_computation.158 | loop fusion | flops 41943040 | bytes 29032460 | tf_op jit(solution)/shard_map/jit(_where)/select_n | solution.py:42
  66.3 7.8 %collective-permute-start.5 = (f32[16,1,32,256]{3,0,2,1:T(8,128)S(1)}, f32[16,1,32,256]{3,0,2,1:T(8,128)S(1)}, u32[]{:S(2)}, u32[]{:S(2)}) collective-permute-start(f32[16,1,32,256]{3,0,2,1:T(8,128)S(1)} %get-tuple-element.40), channel_id=1, source_target_pairs={{0,4},{4,8},{8,12},{12,16},{16,20},{20,24},{24,28},{1,5},{5,9},{9,... | collective-permute-start | bytes 1572872 | tf_op jit(solution)/shard_map/ppermute | solution.py:19
  74.1 1.5 collective-permute-done.5
  77.9 4.9 collective-permute-start.7
  82.8 2.6 collective-permute-done.6
  86.9 24.7 %fusion.87 = f32[16,16,32,256]{3,0,2,1:T(8,128)} fusion(f32[16,16,32,256]{3,0,2,1:T(8,128)} %fusion.81, f32[16,1,32,256]{3,0,2,1:T(8,128)S(1)} %collective-permute-done.4, f32[16,1,32,256]{3,0,2,1:T(8,128)S(1)} %collective-permute-done.5, f32[16,18,1,256]{3,0,2,1:T(8,128)S(1)} %collective-permute-done.7, f32[16,18,1,256]{3,0,2,1:T(8,128)S(1)} %collective-permute-done.6, ...), kind=kLoop, calls=%fused_computation.164 | loop fusion | flops 50331648 | bytes 27983884 | tf_op jit(solution)/shard_map/jit(_where)/select_n | solution.py:42
  114.2 12.9 %collective-permute-start.9 = (f32[16,1,32,256]{3,0,2,1:T(8,128)S(1)}, f32[16,1,32,256]{3,0,2,1:T(8,128)S(1)}, u32[]{:S(2)}, u32[]{:S(2)}) collective-permute-start(f32[16,1,32,256]{3,0,2,1:T(8,128)S(1)} %get-tuple-element.38), channel_id=1, source_target_pairs={{0,4},{4,8},{8,12},{12,16},{16,20},{20,24},{24,28},{1,5},{5,9},{9,... | collective-permute-start | bytes 1572872 | tf_op jit(solution)/shard_map/ppermute | solution.py:19
  127.1 1.5 collective-permute-done.9
  131.0 4.7 collective-permute-start.11
  135.7 2.7 collective-permute-done.10
  139.9 24.7 %fusion.86 = f32[16,16,32,256]{3,0,2,1:T(8,128)} fusion(f32[16,16,32,256]{3,0,2,1:T(8,128)} %fusion.87, f32[16,1,32,256]{3,0,2,1:T(8,128)S(1)} %collective-permute-done.8, f32[16,1,32,256]{3,0,2,1:T(8,128)S(1)} %collective-permute-done.9, f32[16,18,1,256]{3,0,2,1:T(8,128)S(1)} %collective-permute-done.11, ...), kind=kLoop, calls=%fused_computation.163 | loop fusion | flops 50331648 | bytes 27983884 | tf_op jit(solution)/shard_map/jit(_where)/select_n | solution.py:42
  167.2 10.1 %collective-permute-start.13 = (f32[16,1,32,256]{3,0,2,1:T(8,128)S(1)}, f32[16,1,32,256]{3,0,2,1:T(8,128)S(1)}, u32[]{:S(2)}, u32[]{:S(2)}) collective-permute-start(f32[16,1,32,256]{3,0,2,1:T(8,128)S(1)} %get-tuple-element.36), channel_id=1, source_target_pairs={{0,4},{4,8},{8,12},{12,16},{16,20},{20,24},{24,28},{1,5},{5,9},{9,... | collective-permute-start | bytes 1572872 | tf_op jit(solution)/shard_map/ppermute | solution.py:19
  177.3 1.5 collective-permute-done.13
  181.2 4.8 collective-permute-start.15
  186.0 2.7 collective-permute-done.14
  190.2 24.1 %fusion.85 = f32[16,16,32,256]{3,0,2,1:T(8,128)S(1)} fusion(f32[16,16,32,256]{3,0,2,1:T(8,128)} %fusion.86, f32[16,1,32,256]{3,0,2,1:T(8,128)S(1)} %collective-permute-done.12, f32[16,1,32,256]{3,0,2,1:T(8,128)S(1)} %collective-permute-done.13, f32[16,18,1,256]{3,0,2,1:T(8,128)S(1)} %collective-permute-done.15, ...), kind=kLoop, calls=%fused_computation.162 | loop fusion | flops 50331648 | bytes 27983884 | tf_op jit(solution)/shard_map/jit(_where)/select_n | solution.py:42
  215.7 9.8 %collective-permute-start.17 = (f32[16,1,32,256]{3,0,2,1:T(8,128)S(1)}, f32[16,1,32,256]{3,0,2,1:T(8,128)S(1)}, u32[]{:S(2)}, u32[]{:S(2)}) collective-permute-start(f32[16,1,32,256]{3,0,2,1:T(8,128)S(1)} %get-tuple-element.34), channel_id=1, source_target_pairs={{0,4},{4,8},{8,12},{12,16},{16,20},{20,24},{24,28},{1,5},{5,9},{9,... | collective-permute-start | bytes 1572872 | tf_op jit(solution)/shard_map/ppermute | solution.py:19
  225.5 1.5 collective-permute-done.17
  228.4 5.1 collective-permute-start.19
  233.4 2.5 collective-permute-done.18
  237.4 13.0 %fusion.80 = f32[16,16,32,256]{3,0,2,1:T(8,128)} fusion(f32[16,16,32,256]{3,0,2,1:T(8,128)S(1)} %fusion.85, f32[16,1,32,256]{3,0,2,1:T(8,128)S(1)} %collective-permute-done.16, f32[16,1,32,256]{3,0,2,1:T(8,128)S(1)} %collective-permute-done.17, f32[16,18,1,256]{3,0,2,1:T(8,128)S(1)} %collective-permute-done.19, ...), kind=kLoop, calls=%fused_computation.157 | loop fusion | flops 50331648 | bytes 19595276 | tf_op jit(solution)/shard_map/jit(_where)/select_n | solution.py:42
  253.0 9.8 %collective-permute-start.21 = (f32[16,1,32,256]{3,0,2,1:T(8,128)S(1)}, f32[16,1,32,256]{3,0,2,1:T(8,128)S(1)}, u32[]{:S(2)}, u32[]{:S(2)}) collective-permute-start(f32[16,1,32,256]{3,0,2,1:T(8,128)S(1)} %get-tuple-element.32), channel_id=1, source_target_pairs={{0,4},{4,8},{8,12},{12,16},{16,20},{20,24},{24,28},{1,5},{5,9},{9,... | collective-permute-start | bytes 1572872 | tf_op jit(solution)/shard_map/ppermute | solution.py:19
  262.9 1.5 collective-permute-done.21
  266.7 4.8 collective-permute-start.23
  271.6 2.7 collective-permute-done.22
  275.8 22.7 %fusion.84 = f32[16,16,32,256]{3,0,2,1:T(8,128)} fusion(f32[16,16,32,256]{3,0,2,1:T(8,128)S(1)} %fusion.85, f32[16,16,32,256]{3,0,2,1:T(8,128)} %fusion.80, f32[16,1,32,256]{3,0,2,1:T(8,128)S(1)} %collective-permute-done.20, f32[16,1,32,256]{3,0,2,1:T(8,128)S(1)} %collective-permute-done.21, f32[16,18,1,256]{3,0,2,1:T(8,128)S(1)} %collective-permute-done.23, ...), kind=kLoop, calls=%fused_computation.161 | loop fusion | flops 50331648 | bytes 27983884 | tf_op jit(solution)/shard_map/jit(_where)/select_n | solution.py:42
  301.0 11.3 %collective-permute-start.25 = (f32[16,1,32,256]{3,0,2,1:T(8,128)S(1)}, f32[16,1,32,256]{3,0,2,1:T(8,128)S(1)}, u32[]{:S(2)}, u32[]{:S(2)}) collective-permute-start(f32[16,1,32,256]{3,0,2,1:T(8,128)S(1)} %get-tuple-element.30), channel_id=1, source_target_pairs={{0,4},{4,8},{8,12},{12,16},{16,20},{20,24},{24,28},{1,5},{5,9},{9,... | collective-permute-start | bytes 1572872 | tf_op jit(solution)/shard_map/ppermute | solution.py:19
  312.3 1.5 collective-permute-done.25
  316.2 4.7 collective-permute-start.27
  321.6 2.1 collective-permute-done.26
  325.1 22.7 %fusion.83 = f32[16,16,32,256]{3,0,2,1:T(8,128)} fusion(f32[16,16,32,256]{3,0,2,1:T(8,128)S(1)} %fusion.85, f32[16,16,32,256]{3,0,2,1:T(8,128)} %fusion.84, f32[16,1,32,256]{3,0,2,1:T(8,128)S(1)} %collective-permute-done.24, f32[16,1,32,256]{3,0,2,1:T(8,128)S(1)} %collective-permute-done.25, f32[16,18,1,256]{3,0,2,1:T(8,128)S(1)} %collective-permute-done.27, ...), kind=kLoop, calls=%fused_computation.160 | loop fusion | flops 50331648 | bytes 27983884 | tf_op jit(solution)/shard_map/jit(_where)/select_n | solution.py:42
  350.4 13.9 %collective-permute-start.29 = (f32[16,1,32,256]{3,0,2,1:T(8,128)S(1)}, f32[16,1,32,256]{3,0,2,1:T(8,128)S(1)}, u32[]{:S(2)}, u32[]{:S(2)}) collective-permute-start(f32[16,1,32,256]{3,0,2,1:T(8,128)S(1)} %get-tuple-element.28), channel_id=1, source_target_pairs={{0,4},{4,8},{8,12},{12,16},{16,20},{20,24},{24,28},{1,5},{5,9},{9,... | collective-permute-start | bytes 1572872 | tf_op jit(solution)/shard_map/ppermute | solution.py:19
  368.2 4.7 collective-permute-start.31
  373.0 2.7 collective-permute-done.30
  377.2 22.6 %fusion.82 = f32[16,16,32,256]{3,0,2,1:T(8,128)} fusion(f32[16,16,32,256]{3,0,2,1:T(8,128)S(1)} %fusion.85, f32[16,16,32,256]{3,0,2,1:T(8,128)} %fusion.83, f32[16,1,32,256]{3,0,2,1:T(8,128)S(1)} %collective-permute-done.28, f32[16,1,32,256]{3,0,2,1:T(8,128)S(1)} %collective-permute-done.29, f32[16,18,1,256]{3,0,2,1:T(8,128)S(1)} %collective-permute-done.31, ...), kind=kLoop, calls=%fused_computation.159 | loop fusion | flops 50331648 | bytes 27983884 | tf_op jit(solution)/shard_map/jit(_where)/select_n | solution.py:42
  399.8 32.9 %copy.61 = f32[16,16,32,256]{0,3,2,1:T(8,128)} copy(f32[16,16,32,256]{3,0,2,1:T(8,128)} %fusion.82) | data formatting | bytes 16777216 | tf_op jit(solution)/shard_map/jit(_where)/select_n | solution.py:42
  432.7 1.8 gather_fusion
  435.5 39.7 %all-to-all-start = ((f32[32,1,128]{2,1,0:T(1,128)}), f32[32,1,128]{2,1,0:T(1,128)S(1)}, u32[]{:S(2)}, u32[]{:S(2)}) async-start(f32[32,1,128]{2,1,0:T(1,128)} %reshape.93), calls=%async_computation | async-start | bytes 32768 | tf_op jit(solution)/shard_map/all_to_all | solution.py:74
  475.2 11.6 %copy.66 = f32[16,16,32,256]{3,2,1,0:T(8,128)} copy(f32[16,16,32,256]{3,0,2,1:T(8,128)} %fusion.82) | data formatting | bytes 16777216
  488.7 12.2 %psum.14 = f32[16,16]{1,0:T(8,128)S(1)} all-reduce(f32[16,16]{1,0:T(8,128)S(1)} %fusion.109), channel_id=1, replica_groups=mesh['gx'=8,'gy'=4] {'gy'}, use_global_device_ids=true, to_apply=%region_1.2 | all-reduce | flops 256 | bytes 2048 | tf_op jit(solution)/shard_map/psum | solution.py:81
  500.9 12.7 %psum.15 = f32[16,16]{1,0:T(8,128)} all-reduce(f32[16,16]{1,0:T(8,128)S(1)} %psum.14), channel_id=1, replica_groups=mesh['gx'=8,'gy'=4] {'gx'}, use_global_device_ids=true, to_apply=%region_2.3 | all-reduce | flops 256 | bytes 2048 | tf_op jit(solution)/shard_map/psum | solution.py:82
  (85 shorter events, 51.6 us)
Async XLA Ops:
  0.6 15.4 %copy-start = (f32[16,16,32,256]{3,2,1,0:T(8,128)S(1)}, f32[16,16,32,256]{3,2,1,0:T(8,128)}, u32[]{:S(2)}) copy-start(f32[16,16,32,256]{3,2,1,0:T(8,128)} %param.7) | copy-start | bytes 25165828
  0.6 14.4 %copy-start.1 = (f32[16,32,256]{2,1,0:T(8,128)S(1)}, f32[16,32,256]{2,1,0:T(8,128)}, u32[]{:S(2)}) copy-start(f32[16,32,256]{2,1,0:T(8,128)} %param.8) | copy-start | bytes 1572868
  10.7 15.3 %copy-start.2 = (f32[16,16,32,256]{3,0,2,1:T(8,128)}, f32[16,16,32,256]{3,0,2,1:T(8,128)S(1)}, u32[]{:S(2)}) copy-start(f32[16,16,32,256]{3,0,2,1:T(8,128)S(1)} %copy.60) | copy-start | bytes 25165828
  10.8 4.4 collective-permute-start.1
  13.3 12.8 %collective-permute-start = (f32[16,1,32,256]{3,0,2,1:T(8,128)S(1)}, f32[16,1,32,256]{3,0,2,1:T(8,128)S(1)}, u32[]{:S(2)}, u32[]{:S(2)}) collective-permute-start(f32[16,1,32,256]{3,0,2,1:T(8,128)S(1)} %get-tuple-element.42), channel_id=1, source_target_pairs={{4,0},{8,4},{12,8},{16,12},{20,16},{24,20},{28,24},{5,1},{9,5},{13... | collective-permute-start | bytes 1572872 | tf_op jit(solution)/shard_map/ppermute | solution.py:21
  16.0 18.2 %copy-start.5 = (f32[3]{0:T(128)S(1)}, f32[3]{0:T(128)}, u32[]{:S(2)}) copy-start(f32[3]{0:T(128)} %param.9) | copy-start | bytes 40
  28.0 9.0 %collective-permute-start.2 = (f32[16,18,1,256]{3,0,2,1:T(8,128)S(1)}, f32[16,18,1,256]{3,0,2,1:T(8,128)S(1)}, u32[]{:S(2)}, u32[]{:S(2)}) collective-permute-start(f32[16,18,1,256]{3,0,2,1:T(8,128)S(1)} %get-tuple-element.26), channel_id=1, source_target_pairs={{1,0},{2,1},{3,2},{5,4},{6,5},{7,6},{9,8},{10,9},{11,10},{13,12},{... | collective-permute-start | bytes 884744 | tf_op jit(solution)/shard_map/ppermute | solution.py:21
  29.3 9.2 %collective-permute-start.3 = (f32[16,18,1,256]{3,0,2,1:T(8,128)S(1)}, f32[16,18,1,256]{3,0,2,1:T(8,128)S(1)}, u32[]{:S(2)}, u32[]{:S(2)}) collective-permute-start(f32[16,18,1,256]{3,0,2,1:T(8,128)S(1)} %get-tuple-element.27), channel_id=1, source_target_pairs={{0,1},{1,2},{2,3},{4,5},{5,6},{6,7},{8,9},{9,10},{10,11},{12,13},{... | collective-permute-start | bytes 884744 | tf_op jit(solution)/shard_map/ppermute | solution.py:19
  65.0 9.1 %collective-permute-start.4 = (f32[16,1,32,256]{3,0,2,1:T(8,128)S(1)}, f32[16,1,32,256]{3,0,2,1:T(8,128)S(1)}, u32[]{:S(2)}, u32[]{:S(2)}) collective-permute-start(f32[16,1,32,256]{3,0,2,1:T(8,128)S(1)} %get-tuple-element.41), channel_id=1, source_target_pairs={{4,0},{8,4},{12,8},{16,12},{20,16},{24,20},{28,24},{5,1},{9,5},{13... | collective-permute-start | bytes 1572872 | tf_op jit(solution)/shard_map/ppermute | solution.py:21
  66.3 9.3 %collective-permute-start.5 = (f32[16,1,32,256]{3,0,2,1:T(8,128)S(1)}, f32[16,1,32,256]{3,0,2,1:T(8,128)S(1)}, u32[]{:S(2)}, u32[]{:S(2)}) collective-permute-start(f32[16,1,32,256]{3,0,2,1:T(8,128)S(1)} %get-tuple-element.40), channel_id=1, source_target_pairs={{0,4},{4,8},{8,12},{12,16},{16,20},{20,24},{24,28},{1,5},{5,9},{9,... | collective-permute-start | bytes 1572872 | tf_op jit(solution)/shard_map/ppermute | solution.py:19
  76.6 8.8 %collective-permute-start.6 = (f32[16,18,1,256]{3,0,2,1:T(8,128)S(1)}, f32[16,18,1,256]{3,0,2,1:T(8,128)S(1)}, u32[]{:S(2)}, u32[]{:S(2)}) collective-permute-start(f32[16,18,1,256]{3,0,2,1:T(8,128)S(1)} %get-tuple-element.24), channel_id=1, source_target_pairs={{1,0},{2,1},{3,2},{5,4},{6,5},{7,6},{9,8},{10,9},{11,10},{13,12},{... | collective-permute-start | bytes 884744 | tf_op jit(solution)/shard_map/ppermute | solution.py:21
  77.9 8.9 %collective-permute-start.7 = (f32[16,18,1,256]{3,0,2,1:T(8,128)S(1)}, f32[16,18,1,256]{3,0,2,1:T(8,128)S(1)}, u32[]{:S(2)}, u32[]{:S(2)}) collective-permute-start(f32[16,18,1,256]{3,0,2,1:T(8,128)S(1)} %get-tuple-element.25), channel_id=1, source_target_pairs={{0,1},{1,2},{2,3},{4,5},{5,6},{6,7},{8,9},{9,10},{10,11},{12,13},{... | collective-permute-start | bytes 884744 | tf_op jit(solution)/shard_map/ppermute | solution.py:19
  112.9 14.2 %collective-permute-start.8 = (f32[16,1,32,256]{3,0,2,1:T(8,128)S(1)}, f32[16,1,32,256]{3,0,2,1:T(8,128)S(1)}, u32[]{:S(2)}, u32[]{:S(2)}) collective-permute-start(f32[16,1,32,256]{3,0,2,1:T(8,128)S(1)} %get-tuple-element.39), channel_id=1, source_target_pairs={{4,0},{8,4},{12,8},{16,12},{20,16},{24,20},{28,24},{5,1},{9,5},{13... | collective-permute-start | bytes 1572872 | tf_op jit(solution)/shard_map/ppermute | solution.py:21
  114.2 14.4 %collective-permute-start.9 = (f32[16,1,32,256]{3,0,2,1:T(8,128)S(1)}, f32[16,1,32,256]{3,0,2,1:T(8,128)S(1)}, u32[]{:S(2)}, u32[]{:S(2)}) collective-permute-start(f32[16,1,32,256]{3,0,2,1:T(8,128)S(1)} %get-tuple-element.38), channel_id=1, source_target_pairs={{0,4},{4,8},{8,12},{12,16},{16,20},{20,24},{24,28},{1,5},{5,9},{9,... | collective-permute-start | bytes 1572872 | tf_op jit(solution)/shard_map/ppermute | solution.py:19
  129.7 8.8 %collective-permute-start.10 = (f32[16,18,1,256]{3,0,2,1:T(8,128)S(1)}, f32[16,18,1,256]{3,0,2,1:T(8,128)S(1)}, u32[]{:S(2)}, u32[]{:S(2)}) collective-permute-start(f32[16,18,1,256]{3,0,2,1:T(8,128)S(1)} %get-tuple-element.22), channel_id=1, source_target_pairs={{1,0},{2,1},{3,2},{5,4},{6,5},{7,6},{9,8},{10,9},{11,10},{13,12},{... | collective-permute-start | bytes 884744 | tf_op jit(solution)/shard_map/ppermute | solution.py:21
  131.0 8.9 %collective-permute-start.11 = (f32[16,18,1,256]{3,0,2,1:T(8,128)S(1)}, f32[16,18,1,256]{3,0,2,1:T(8,128)S(1)}, u32[]{:S(2)}, u32[]{:S(2)}) collective-permute-start(f32[16,18,1,256]{3,0,2,1:T(8,128)S(1)} %get-tuple-element.23), channel_id=1, source_target_pairs={{0,1},{1,2},{2,3},{4,5},{5,6},{6,7},{8,9},{9,10},{10,11},{12,13},{... | collective-permute-start | bytes 884744 | tf_op jit(solution)/shard_map/ppermute | solution.py:19
  165.9 11.4 %collective-permute-start.12 = (f32[16,1,32,256]{3,0,2,1:T(8,128)S(1)}, f32[16,1,32,256]{3,0,2,1:T(8,128)S(1)}, u32[]{:S(2)}, u32[]{:S(2)}) collective-permute-start(f32[16,1,32,256]{3,0,2,1:T(8,128)S(1)} %get-tuple-element.37), channel_id=1, source_target_pairs={{4,0},{8,4},{12,8},{16,12},{20,16},{24,20},{28,24},{5,1},{9,5},{13... | collective-permute-start | bytes 1572872 | tf_op jit(solution)/shard_map/ppermute | solution.py:21
  167.2 11.6 %collective-permute-start.13 = (f32[16,1,32,256]{3,0,2,1:T(8,128)S(1)}, f32[16,1,32,256]{3,0,2,1:T(8,128)S(1)}, u32[]{:S(2)}, u32[]{:S(2)}) collective-permute-start(f32[16,1,32,256]{3,0,2,1:T(8,128)S(1)} %get-tuple-element.36), channel_id=1, source_target_pairs={{0,4},{4,8},{8,12},{12,16},{16,20},{20,24},{24,28},{1,5},{5,9},{9,... | collective-permute-start | bytes 1572872 | tf_op jit(solution)/shard_map/ppermute | solution.py:19
  179.9 8.9 %collective-permute-start.14 = (f32[16,18,1,256]{3,0,2,1:T(8,128)S(1)}, f32[16,18,1,256]{3,0,2,1:T(8,128)S(1)}, u32[]{:S(2)}, u32[]{:S(2)}) collective-permute-start(f32[16,18,1,256]{3,0,2,1:T(8,128)S(1)} %get-tuple-element.20), channel_id=1, source_target_pairs={{1,0},{2,1},{3,2},{5,4},{6,5},{7,6},{9,8},{10,9},{11,10},{13,12},{... | collective-permute-start | bytes 884744 | tf_op jit(solution)/shard_map/ppermute | solution.py:21
  181.2 9.1 %collective-permute-start.15 = (f32[16,18,1,256]{3,0,2,1:T(8,128)S(1)}, f32[16,18,1,256]{3,0,2,1:T(8,128)S(1)}, u32[]{:S(2)}, u32[]{:S(2)}) collective-permute-start(f32[16,18,1,256]{3,0,2,1:T(8,128)S(1)} %get-tuple-element.21), channel_id=1, source_target_pairs={{0,1},{1,2},{2,3},{4,5},{5,6},{6,7},{8,9},{9,10},{10,11},{12,13},{... | collective-permute-start | bytes 884744 | tf_op jit(solution)/shard_map/ppermute | solution.py:19
  214.4 11.1 %collective-permute-start.16 = (f32[16,1,32,256]{3,0,2,1:T(8,128)S(1)}, f32[16,1,32,256]{3,0,2,1:T(8,128)S(1)}, u32[]{:S(2)}, u32[]{:S(2)}) collective-permute-start(f32[16,1,32,256]{3,0,2,1:T(8,128)S(1)} %get-tuple-element.35), channel_id=1, source_target_pairs={{4,0},{8,4},{12,8},{16,12},{20,16},{24,20},{28,24},{5,1},{9,5},{13... | collective-permute-start | bytes 1572872 | tf_op jit(solution)/shard_map/ppermute | solution.py:21
  215.7 11.3 %collective-permute-start.17 = (f32[16,1,32,256]{3,0,2,1:T(8,128)S(1)}, f32[16,1,32,256]{3,0,2,1:T(8,128)S(1)}, u32[]{:S(2)}, u32[]{:S(2)}) collective-permute-start(f32[16,1,32,256]{3,0,2,1:T(8,128)S(1)} %get-tuple-element.34), channel_id=1, source_target_pairs={{0,4},{4,8},{8,12},{12,16},{16,20},{20,24},{24,28},{1,5},{5,9},{9,... | collective-permute-start | bytes 1572872 | tf_op jit(solution)/shard_map/ppermute | solution.py:19
  227.1 8.9 %collective-permute-start.18 = (f32[16,18,1,256]{3,0,2,1:T(8,128)S(1)}, f32[16,18,1,256]{3,0,2,1:T(8,128)S(1)}, u32[]{:S(2)}, u32[]{:S(2)}) collective-permute-start(f32[16,18,1,256]{3,0,2,1:T(8,128)S(1)} %get-tuple-element.18), channel_id=1, source_target_pairs={{1,0},{2,1},{3,2},{5,4},{6,5},{7,6},{9,8},{10,9},{11,10},{13,12},{... | collective-permute-start | bytes 884744 | tf_op jit(solution)/shard_map/ppermute | solution.py:21
  228.4 9.1 %collective-permute-start.19 = (f32[16,18,1,256]{3,0,2,1:T(8,128)S(1)}, f32[16,18,1,256]{3,0,2,1:T(8,128)S(1)}, u32[]{:S(2)}, u32[]{:S(2)}) collective-permute-start(f32[16,18,1,256]{3,0,2,1:T(8,128)S(1)} %get-tuple-element.19), channel_id=1, source_target_pairs={{0,1},{1,2},{2,3},{4,5},{5,6},{6,7},{8,9},{9,10},{10,11},{12,13},{... | collective-permute-start | bytes 884744 | tf_op jit(solution)/shard_map/ppermute | solution.py:19
  251.7 11.1 %collective-permute-start.20 = (f32[16,1,32,256]{3,0,2,1:T(8,128)S(1)}, f32[16,1,32,256]{3,0,2,1:T(8,128)S(1)}, u32[]{:S(2)}, u32[]{:S(2)}) collective-permute-start(f32[16,1,32,256]{3,0,2,1:T(8,128)S(1)} %get-tuple-element.33), channel_id=1, source_target_pairs={{4,0},{8,4},{12,8},{16,12},{20,16},{24,20},{28,24},{5,1},{9,5},{13... | collective-permute-start | bytes 1572872 | tf_op jit(solution)/shard_map/ppermute | solution.py:21
  253.0 11.3 %collective-permute-start.21 = (f32[16,1,32,256]{3,0,2,1:T(8,128)S(1)}, f32[16,1,32,256]{3,0,2,1:T(8,128)S(1)}, u32[]{:S(2)}, u32[]{:S(2)}) collective-permute-start(f32[16,1,32,256]{3,0,2,1:T(8,128)S(1)} %get-tuple-element.32), channel_id=1, source_target_pairs={{0,4},{4,8},{8,12},{12,16},{16,20},{20,24},{24,28},{1,5},{5,9},{9,... | collective-permute-start | bytes 1572872 | tf_op jit(solution)/shard_map/ppermute | solution.py:19
  265.4 8.9 %collective-permute-start.22 = (f32[16,18,1,256]{3,0,2,1:T(8,128)S(1)}, f32[16,18,1,256]{3,0,2,1:T(8,128)S(1)}, u32[]{:S(2)}, u32[]{:S(2)}) collective-permute-start(f32[16,18,1,256]{3,0,2,1:T(8,128)S(1)} %get-tuple-element.16), channel_id=1, source_target_pairs={{1,0},{2,1},{3,2},{5,4},{6,5},{7,6},{9,8},{10,9},{11,10},{13,12},{... | collective-permute-start | bytes 884744 | tf_op jit(solution)/shard_map/ppermute | solution.py:21
  266.7 9.1 %collective-permute-start.23 = (f32[16,18,1,256]{3,0,2,1:T(8,128)S(1)}, f32[16,18,1,256]{3,0,2,1:T(8,128)S(1)}, u32[]{:S(2)}, u32[]{:S(2)}) collective-permute-start(f32[16,18,1,256]{3,0,2,1:T(8,128)S(1)} %get-tuple-element.17), channel_id=1, source_target_pairs={{0,1},{1,2},{2,3},{4,5},{5,6},{6,7},{8,9},{9,10},{10,11},{12,13},{... | collective-permute-start | bytes 884744 | tf_op jit(solution)/shard_map/ppermute | solution.py:19
  299.7 12.6 %collective-permute-start.24 = (f32[16,1,32,256]{3,0,2,1:T(8,128)S(1)}, f32[16,1,32,256]{3,0,2,1:T(8,128)S(1)}, u32[]{:S(2)}, u32[]{:S(2)}) collective-permute-start(f32[16,1,32,256]{3,0,2,1:T(8,128)S(1)} %get-tuple-element.31), channel_id=1, source_target_pairs={{4,0},{8,4},{12,8},{16,12},{20,16},{24,20},{28,24},{5,1},{9,5},{13... | collective-permute-start | bytes 1572872 | tf_op jit(solution)/shard_map/ppermute | solution.py:21
  301.0 12.8 %collective-permute-start.25 = (f32[16,1,32,256]{3,0,2,1:T(8,128)S(1)}, f32[16,1,32,256]{3,0,2,1:T(8,128)S(1)}, u32[]{:S(2)}, u32[]{:S(2)}) collective-permute-start(f32[16,1,32,256]{3,0,2,1:T(8,128)S(1)} %get-tuple-element.30), channel_id=1, source_target_pairs={{0,4},{4,8},{8,12},{12,16},{16,20},{20,24},{24,28},{1,5},{5,9},{9,... | collective-permute-start | bytes 1572872 | tf_op jit(solution)/shard_map/ppermute | solution.py:19
  314.9 8.8 %collective-permute-start.26 = (f32[16,18,1,256]{3,0,2,1:T(8,128)S(1)}, f32[16,18,1,256]{3,0,2,1:T(8,128)S(1)}, u32[]{:S(2)}, u32[]{:S(2)}) collective-permute-start(f32[16,18,1,256]{3,0,2,1:T(8,128)S(1)} %get-tuple-element.14), channel_id=1, source_target_pairs={{1,0},{2,1},{3,2},{5,4},{6,5},{7,6},{9,8},{10,9},{11,10},{13,12},{... | collective-permute-start | bytes 884744 | tf_op jit(solution)/shard_map/ppermute | solution.py:21
  316.2 8.9 %collective-permute-start.27 = (f32[16,18,1,256]{3,0,2,1:T(8,128)S(1)}, f32[16,18,1,256]{3,0,2,1:T(8,128)S(1)}, u32[]{:S(2)}, u32[]{:S(2)}) collective-permute-start(f32[16,18,1,256]{3,0,2,1:T(8,128)S(1)} %get-tuple-element.15), channel_id=1, source_target_pairs={{0,1},{1,2},{2,3},{4,5},{5,6},{6,7},{8,9},{9,10},{10,11},{12,13},{... | collective-permute-start | bytes 884744 | tf_op jit(solution)/shard_map/ppermute | solution.py:19
  321.6 42.8 %copy-start.7 = (s32[1,1,128,1]{2,3,1,0:T(1,128)S(1)}, s32[1,1,128,1]{2,3,1,0:T(1,128)}, u32[]{:S(2)}) copy-start(s32[1,1,128,1]{2,3,1,0:T(1,128)} %param.11) | copy-start | bytes 1540
  321.6 42.9 %copy-start.6 = (s32[1,1,128]{2,1,0:T(1,128)S(1)}, s32[1,1,128]{2,1,0:T(1,128)}, u32[]{:S(2)}) copy-start(s32[1,1,128]{2,1,0:T(1,128)} %param.10) | copy-start | bytes 1540
  349.1 15.5 %collective-permute-start.28 = (f32[16,1,32,256]{3,0,2,1:T(8,128)S(1)}, f32[16,1,32,256]{3,0,2,1:T(8,128)S(1)}, u32[]{:S(2)}, u32[]{:S(2)}) collective-permute-start(f32[16,1,32,256]{3,0,2,1:T(8,128)S(1)} %get-tuple-element.29), channel_id=1, source_target_pairs={{4,0},{8,4},{12,8},{16,12},{20,16},{24,20},{28,24},{5,1},{9,5},{13... | collective-permute-start | bytes 1572872 | tf_op jit(solution)/shard_map/ppermute | solution.py:21
  350.4 15.4 %collective-permute-start.29 = (f32[16,1,32,256]{3,0,2,1:T(8,128)S(1)}, f32[16,1,32,256]{3,0,2,1:T(8,128)S(1)}, u32[]{:S(2)}, u32[]{:S(2)}) collective-permute-start(f32[16,1,32,256]{3,0,2,1:T(8,128)S(1)} %get-tuple-element.28), channel_id=1, source_target_pairs={{0,4},{4,8},{8,12},{12,16},{16,20},{20,24},{24,28},{1,5},{5,9},{9,... | collective-permute-start | bytes 1572872 | tf_op jit(solution)/shard_map/ppermute | solution.py:19
  366.9 8.8 %collective-permute-start.30 = (f32[16,18,1,256]{3,0,2,1:T(8,128)S(1)}, f32[16,18,1,256]{3,0,2,1:T(8,128)S(1)}, u32[]{:S(2)}, u32[]{:S(2)}) collective-permute-start(f32[16,18,1,256]{3,0,2,1:T(8,128)S(1)} %get-tuple-element.12), channel_id=1, source_target_pairs={{1,0},{2,1},{3,2},{5,4},{6,5},{7,6},{9,8},{10,9},{11,10},{13,12},{... | collective-permute-start | bytes 884744 | tf_op jit(solution)/shard_map/ppermute | solution.py:21
  368.2 8.9 %collective-permute-start.31 = (f32[16,18,1,256]{3,0,2,1:T(8,128)S(1)}, f32[16,18,1,256]{3,0,2,1:T(8,128)S(1)}, u32[]{:S(2)}, u32[]{:S(2)}) collective-permute-start(f32[16,18,1,256]{3,0,2,1:T(8,128)S(1)} %get-tuple-element.13), channel_id=1, source_target_pairs={{0,1},{1,2},{2,3},{4,5},{5,6},{6,7},{8,9},{9,10},{10,11},{12,13},{... | collective-permute-start | bytes 884744 | tf_op jit(solution)/shard_map/ppermute | solution.py:19
  399.8 34.8 %copy-start.4 = (f32[1,1,128,16]{2,3,1,0:T(8,128)S(1)}, f32[1,1,128,16]{2,3,1,0:T(8,128)}, u32[]{:S(2)}) copy-start(f32[1,1,128,16]{2,3,1,0:T(8,128)} %param.13) | copy-start | bytes 24580
  435.5 51.3 %all-to-all-start = ((f32[32,1,128]{2,1,0:T(1,128)}), f32[32,1,128]{2,1,0:T(1,128)S(1)}, u32[]{:S(2)}, u32[]{:S(2)}) async-start(f32[32,1,128]{2,1,0:T(1,128)} %reshape.93), calls=%async_computation | async-start | bytes 32768 | tf_op jit(solution)/shard_map/all_to_all | solution.py:74
  488.4 25.2 %copy-start.3 = (f32[16,16]{1,0:T(8,128)}, f32[16,16]{1,0:T(8,128)S(1)}, u32[]{:S(2)}) copy-start(f32[16,16]{1,0:T(8,128)S(1)} %convolution_bitcast_fusion) | copy-start | bytes 3076
